TPU v7x, 32 devices: a whole 2x2x4 slice. The times are simulated.
32 devices in a mesh: row: 8 (over z, x), col: 4 (over y, core).
Axes of the slice: x: 2, y: 2, z: 4, core: 2. Of those that a mesh axis runs over, the one named last changes fastest.
Arguments:
- samples: float32 [4096, 512], P(('row', 'col')), may hold values from -8 to 8
- labels: int32 [4096, 256], P(('row', 'col')), may hold values from -1 to 1, as said below
Outputs:
- statistic: float32 [256], replicated
- proof: float32 [4096], P(('row', 'col'))
- p_value: float32 [], replicated
Inputs may be any that keep to these rules, and one draw needn't show every extreme that they name: `labels`: every column holds exactly 2048 entries +1 and 2048 entries -1.
All inputs are finite; a program needn't handle non-finite values.
Results may differ from a plain program's by a relative error of at most 0.0003.
Values sent between devices are 32-bit elements; how exact they have to be, the bound alone decides.
A program may use at most 64 MiB of HBM per device.

v0:
```python
import math

import jax
import jax.numpy as jnp
from jax import lax
from jax.sharding import PartitionSpec as P


def tile_terms(xr, lr, gr, xc, lc, gc, width):
    norm_rows = jnp.sum(xr * xr, 1)
    norm_cols = jnp.sum(xc * xc, 1)
    dots = lax.dot_general(
        xr,
        xc,
        (((1,), (1,)), ((), ())),
        precision=lax.Precision.HIGHEST,
        preferred_element_type=jnp.float32,
    )
    dist = jnp.maximum(norm_rows[:, None] + norm_cols[None, :] - 2.0 * dots, 0.0)
    kern = jnp.where(gr[:, None] == gc[None, :], 0.0, jnp.exp(-dist / (2.0 * width)))
    proj = jnp.dot(kern, lc, precision=lax.Precision.HIGHEST, preferred_element_type=jnp.float32)
    return (proj[:, 0], jnp.sum(lr * proj, 0), jnp.sum(kern))


def rows_terms(row_x, row_l, row_ids, col_x, col_l, col_ids, width):
    block = row_x.shape[0]
    perms = row_l.shape[1]
    tile = math.gcd(block, 512)
    count = block // tile

    def one(args):
        xr, lr, gr = args
        return tile_terms(xr, lr, gr, col_x, col_l, col_ids, width)

    wit, quad, tot = lax.map(
        one,
        (
            row_x.reshape(count, tile, width),
            row_l.reshape(count, tile, perms),
            row_ids.reshape(count, tile),
        ),
    )
    return (wit.reshape(block), jnp.sum(quad, 0), jnp.sum(tot))


def shards(samples, labels):
    shard = samples.shape[0]
    width = samples.shape[1]
    n_row = lax.axis_size("row")
    n_col = lax.axis_size("col")
    block = shard * n_col
    labs = labels.astype(jnp.float32)
    row_x, row_l = (
        lax.all_gather(samples, "col", axis=0, tiled=True),
        lax.all_gather(labs, "col", axis=0, tiled=True),
    )
    row_ids = lax.axis_index("row") * block + jnp.arange(block, dtype=jnp.int32)
    col_base = lax.axis_index("col") * shard
    col_x, col_l = (
        lax.all_gather(samples, "row", axis=0, tiled=True),
        lax.all_gather(labs, "row", axis=0, tiled=True),
    )
    positions = jnp.arange(shard * n_row, dtype=jnp.int32)
    col_ids = positions // shard * block + col_base + positions % shard
    wit, quad, total = rows_terms(row_x, row_l, row_ids, col_x, col_l, col_ids, width)
    all_rows = shard * n_row * n_col
    own_wit = lax.psum_scatter(wit, "col", scatter_dimension=0, tiled=True)
    proof = own_wit / jnp.sqrt(jnp.float32(all_rows))
    quad, total = lax.psum((quad, total), ("row", "col"))
    half = all_rows / 2.0
    statistic = (
        total / (2.0 * half * (half - 1.0))
        + (2.0 * half - 1.0) / (2.0 * half * (half - 1.0)) * quad
    )
    p_value = jnp.mean(jax.nn.sigmoid(4.0 * (statistic[1:] - statistic[0])))
    return (statistic, proof, p_value)


def solution(mesh):
    placed = (P(("row", "col"), None), P(("row", "col"), None))
    return jax.shard_map(
        shards, mesh=mesh, in_specs=placed, out_specs=(P(), P(("row", "col")), P()), check_vma=False
    )
```

profile of v0, /device:TPU:0, one launch (start us, length us, event | category | flops | bytes accessed | tf_op | source)
XLA Modules:
  0.0 181.0 jit_solution(812595770687839186)
XLA Ops:
  7.2 0.0 all-gather.4.cloned.1.call-start
  7.2 0.7 all-gather.4.cloned.1.call-update
  7.9 0.0 all-gather.6.cloned.1.call-start
  7.9 0.7 all-gather.6.cloned.1.call-update
  8.6 0.0 all-gather.8.cloned.1.call-start
  8.7 1.0 copy.6
  9.7 0.7 convert_element_type.3
  10.4 0.0 all-gather.8.cloned.1.call-update
  10.4 1.2 dynamic-slice.3
  12.3 8.9 %all_gather.14 = f32[512,256]{0,1:T(8,128)S(1)} all-gather(f32[128,256]{0,1:T(8,128)} %convert_element_type.3), channel_id=1, replica_groups=mesh['row'=8,'col'=4] {'col'}, dimensions={0}, use_global_device_ids=true | all-gather | bytes 655360 | tf_op jit(solution)/shard_map/all_gather | solution.py:55
  21.2 7.8 %all-gather.4.cloned.1.call-done = f32[512,512]{1,0:T(8,128)} async-done(((f32[128,512]{1,0:T(8,128)}), f32[512,512]{1,0:T(8,128)}) %all-gather.4.cloned.1.call-update) | async-done | bytes 1048592 | tf_op jit(solution)/shard_map/all_gather | solution.py:54
  29.0 1.4 multiply_reduce_fusion.1
  30.4 49.9 %all-gather.6.cloned.1.call-done = f32[1024,512]{1,0:T(8,128)} async-done(((f32[128,512]{1,0:T(8,128)}), f32[1024,512]{1,0:T(8,128)}) %all-gather.6.cloned.1.call-update) | async-done | bytes 2097168 | tf_op jit(solution)/shard_map/all_gather | solution.py:60
  80.2 0.0 copy-start
  80.2 2.0 %multiply_reduce_fusion = f32[1024]{0:T(1024)S(1)} fusion(f32[1024,512]{1,0:T(8,128)} %all-gather.6.cloned.1.call-done), kind=kLoop, calls=%fused_computation.1 | loop fusion | flops 1047552 | bytes 2101248 | tf_op jit(solution)/shard_map/while/body/eval_jaxpr/reduce_sum | solution.py:11
  82.2 0.3 copy-done
  82.5 5.9 %fusion.11 = (f32[]{:T(128)}, f32[512,1024]{1,0:T(8,128)S(1)}) fusion(f32[512,512]{1,0:T(8,128)} %all-gather.4.cloned.1.call-done, f32[1024,512]{1,0:T(8,128)S(1)} %copy-done, f32[1024]{0:T(1024)S(1)} %multiply_reduce_fusion, f32[512]{0:T(512)S(1)} %multiply_reduce_fusion.1, s32[1024]{0:T(1024)S(1)} %fusion.8, s32[512]{0:T(512)S(1)} %iota_add_fusion), kind=kOutput, calls=%fused_computation.23 | convolution fusion | flops 3225944064 | bytes 5255172 | tf_op jit(solution)/shard_map/while/body/eval_jaxpr/dot_general | solution.py:12
  88.4 31.9 %all-gather.8.cloned.1.call-done = f32[1024,256]{0,1:T(8,128)} async-done(((f32[128,256]{0,1:T(8,128)}), f32[1024,256]{0,1:T(8,128)}) %all-gather.8.cloned.1.call-update) | async-done | bytes 1048592 | tf_op jit(solution)/shard_map/all_gather | solution.py:61
  120.2 3.3 %multiply_reduce_fusion.2 = (f32[256]{0:T(256)S(1)}, f32[512,256]{0,1:T(8,128)S(1)}) fusion(f32[512,256]{0,1:T(8,128)S(1)} %all_gather.14, f32[512,1024]{1,0:T(8,128)S(1)} %get-tuple-element.28, f32[1024,256]{0,1:T(8,128)} %all-gather.8.cloned.1.call-done), kind=kOutput, calls=%fused_computation.3 | convolution fusion | flops 1610874624 | bytes 4195328 | tf_op jit(solution)/shard_map/while/body/eval_jaxpr/dot_general | solution.py:21
  123.5 40.1 %all-reduce.1 = (f32[256]{0:T(256)S(1)}, f32[]{:T(128)}) all-reduce(f32[256]{0:T(256)S(1)} %get-tuple-element.25, f32[]{:T(128)} %get-tuple-element.27), channel_id=1, replica_groups=mesh['row'=8,'col'=4] {'row','col'}, use_global_device_ids=true, to_apply=%region_5.6 | all-reduce | flops 257 | bytes 2056 | tf_op jit(solution)/shard_map/psum | solution.py:69
  164.3 0.0 copy-start.1
  164.3 0.5 slice.12
  164.8 1.3 fusion.10
  166.1 6.0 %all-reduce = f32[512]{0:T(512)S(1)} all-reduce(f32[512]{0:T(512)S(1)} %bitcast.7), channel_id=2, replica_groups=mesh['row'=8,'col'=4] {'col'}, use_global_device_ids=true, to_apply=%region_6.7.clone | all-reduce | flops 512 | bytes 4096
  172.8 0.6 dynamic-slice_multiply_fusion
  173.3 0.0 copy-done.1
  (4 shorter events, 0.0 us)
Async XLA Ops:
  7.2 21.8 %all-gather.4.cloned.1.call-start = ((), (), s32[]{:S(2)}) async-start(), calls=%async_computation | async-start | bytes 1310720 | tf_op jit(solution)/shard_map/all_gather | solution.py:54
  7.9 72.3 %all-gather.6.cloned.1.call-start = ((), (), s32[]{:S(2)}) async-start(), calls=%async_computation.1 | async-start | bytes 2359296 | tf_op jit(solution)/shard_map/all_gather | solution.py:60
  8.6 111.6 %all-gather.8.cloned.1.call-start = ((), (), s32[]{:S(2)}) async-start(), calls=%async_computation.2 | async-start | bytes 1179648 | tf_op jit(solution)/shard_map/all_gather | solution.py:61
  80.2 2.2 %copy-start = (f32[1024,512]{1,0:T(8,128)S(1)}, f32[1024,512]{1,0:T(8,128)}, u32[]{:S(2)}) copy-start(f32[1024,512]{1,0:T(8,128)} %all-gather.6.cloned.1.call-done) | copy-start | bytes 6291460
  164.3 9.1 %copy-start.1 = (f32[256]{0:T(256)}, f32[256]{0:T(256)S(1)}, u32[]{:S(2)}) copy-start(f32[256]{0:T(256)S(1)} %multiply_add_fusion) | copy-start | bytes 3076
Sparse Core Ops, SparseCore 0:
  9.5 19.4 all-gather.3
  31.1 49.0 all-gather.5
  82.3 37.9 all-gather.7
where the time goes:
time: 181 us
  waiting for transfers between devices  90.9 us (50%)
  blocking collectives  54.9 us (30%)
  between operations  16.9 us (9%)
  matrix products  9.2 us (5%)
  other arithmetic  5.92 us (3%)
  local copies, waits for them, and re-layouts  3.02 us (2%)
    all_gather x1, waiting for transfers between devices, shards(): lax.all_gather(samples, 'row', axis=0, tiled=True)  49.9 us
    psum x1, blocking collectives, shards(): quad, total = lax.psum((quad, total), ('row', 'col'))  40.1 us
    all_gather x1, waiting for transfers between devices, shards(): lax.all_gather(labs, 'row', axis=0, tiled=True)  31.9 us
    all_gather x1, blocking collectives, shards(): lax.all_gather(labs, 'col', axis=0, tiled=True)  8.89 us
    all_gather x1, waiting for transfers between devices, shards(): lax.all_gather(samples, 'col', axis=0, tiled=True)  7.79 us
    unnamed x1, blocking collectives  5.98 us
    dot_general x1, matrix products, tile_terms(): lax.dot_general(xr, xc, (((1,), (1,)), ((), ())), precision=lax.Precision...  5.93 us
  transfers between devices with their start and end apart: 3, of which 3 were waited for; matrix products, arithmetic and copies ran while one was open for 7% of the time, Pallas kernels for 0%

commit v1 on v0

v1 whole, which is shorter than its diff:
```python
import functools
import math

import jax
import jax.numpy as jnp
from jax import lax
from jax.experimental import pallas as pl
from jax.experimental.pallas import tpu as pltpu
from jax.sharding import PartitionSpec as P

MESH = pl.DeviceIdType.MESH
F32 = jnp.float32
BF16 = jnp.bfloat16
CHUNKS = 4
PARTS = 2

ROUTES = {1: {}, 2: {0: (1, 1)}, 4: {0: (1, 3), 2: (-1, 1), 3: (-1, 2)}}


def nt(a, b):
    return lax.dot_general(a, b, (((1,), (1,)), ((), ())), preferred_element_type=F32)


def nn(a, b):
    return lax.dot_general(a, b, (((1,), (0,)), ((), ())), preferred_element_type=F32)


def split(v):
    hi = v.astype(BF16)
    return hi, (v - hi.astype(F32)).astype(BF16)


def to_row(column):
    n = column.shape[0]
    return jnp.transpose(jnp.broadcast_to(column, (n, n)))[0:1, :]


class Plan:
    def __init__(self, n_row, n_col, blk, width, perms):
        self.nz = math.gcd(n_row, 4)
        self.nx = n_row // self.nz
        self.nk = math.gcd(n_col, 2)
        self.ny = n_col // self.nk
        self.n_col = n_col
        self.n_lev = self.nx * n_col
        self.blk, self.width, self.perms = blk, width, perms
        self.group = math.gcd(self.n_lev, 4)
        self.rows = blk * n_row * n_col


def kernel(pn, n_send, x_ref, l_ref, stat_ref, proof_ref, p_ref, RX, RL, CX, CL, RHI, RLO, RLB, NR,
           ROWP, QUAD, TOT, COLP, S1, R1, S2, R2, send, lev_sem, z_sem, s1_send, s1_recv, s2_send, s2_recv):
    nx, ny, nz, nk, n_col, n_lev, blk = pn.nx, pn.ny, pn.nz, pn.nk, pn.n_col, pn.n_lev, pn.blk
    row, col = lax.axis_index("row"), lax.axis_index("col")
    z, x = row // nx, row % nx
    y, core = col // nk, col % nk
    me = x * n_col + col
    routes = ROUTES[nz]
    pending = []

    def lev_of(xx, yy, kk):
        return xx * n_col + yy * nk + kk

    def dev(zz, xx, yy, kk):
        return (zz * nx + xx, yy * nk + kk)

    def lev_dev(k):
        return (z * nx + k // n_col, k % n_col)

    barrier = pltpu.get_barrier_semaphore()
    for d in range(1, n_lev):
        pl.semaphore_signal(barrier, inc=1, device_id=lev_dev((me + d) % n_lev), device_id_type=MESH)
    for d in range(1, nz):
        pl.semaphore_signal(barrier, inc=1, device_id=dev((z + d) % nz, x, y, core), device_id_type=MESH)
    pl.semaphore_wait(barrier, n_lev - 1 + nz - 1)

    counter = [0]

    def new_sem():
        counter[0] += 1
        return send.at[counter[0] - 1]

    half = blk // PARTS
    piece = blk // CHUNKS

    def lev_copy(k, part, target, own, sem):
        r = pl.ds(part * half, half)
        out = []
        for i, (src, dst) in enumerate(((x_ref, RX), (l_ref, RL))):
            s = src.at[r] if own else dst.at[k, r]
            out.append(pltpu.make_async_remote_copy(
                src_ref=s, dst_ref=dst.at[k, r], send_sem=new_sem() if sem else send.at[0],
                recv_sem=lev_sem.at[k, part * 2 + i], device_id=target, device_id_type=MESH))
        return out

    def lev_send(k, part, target, own=False):
        for c in lev_copy(k, part, target, own, True):
            c.start()
            pending.append(c)

    def lev_wait(k, part):
        for c in lev_copy(k, part, (row, col), False, False):
            c.wait_recv()

    def z_copy(b, ch, target, own, sems):
        r = pl.ds(ch * piece, piece)
        out = []
        for i, (src, dst) in enumerate(((x_ref, CX), (l_ref, CL))):
            s = src.at[r] if own else dst.at[b, r]
            out.append(pltpu.make_async_remote_copy(
                src_ref=s, dst_ref=dst.at[b, r], send_sem=sems[i],
                recv_sem=z_sem.at[b, ch * 2 + i], device_id=target, device_id_type=MESH))
        return out

    z_pending = []

    def z_send(b, ch, at, own):
        sems = [new_sem(), new_sem()]
        to = at + routes[b][0]

        @pl.when(z == at)
        def _():
            for c in z_copy(b, ch, dev(to, x, y, core), own, sems):
                c.start()
        z_pending.append((b, ch, at, own, sems))

    def z_event(b, ch, hop):
        at = b + routes[b][0] * hop

        @pl.when(z == at)
        def _():
            for c in z_copy(b, ch, (row, col), False, [send.at[0]] * 2):
                c.wait_recv()
        if hop < routes[b][1]:
            z_send(b, ch, at, False)

    def xm(d):
        return (x + d) % nx

    def ym(d):
        return (y + d) % ny

    other = (core + 1) % nk
    A, B = 0, 1
    for ch in range(CHUNKS):
        for b in routes:
            z_send(b, ch, b, True)
    for d in range(1, nx):
        lev_send(me, A, dev(z, xm(d), y, core), True)
    for d in range(1, ny):
        lev_send(me, B, dev(z, x, ym(d), core), True)
    for d in range(1, nx):
        lev_send(me, B, dev(z, xm(d), y, core), True)
    for d in range(1, ny):
        lev_send(me, A, dev(z, x, ym(d), core), True)
    if nk > 1:
        for part in (A, B):
            lev_send(me, part, dev(z, x, y, other), True)

    def prep(k, xv, lv):
        rows = pl.ds(pl.multiple_of(k * blk, blk), blk)
        hi, lo = split(xv)
        RHI[rows, :] = hi
        RLO[rows, :] = lo
        RLB[rows, :] = lv.astype(F32).astype(BF16)
        NR[:, rows] = to_row(jnp.sum(xv * xv, axis=1, keepdims=True))

    prep(me, x_ref[...], l_ref[...])

    def hops(b):
        return routes[b][1]

    def z_round(hop, ch):
        for b in routes:
            if hop <= hops(b):
                z_event(b, ch, hop)

    z_round(1, 0)
    for d in range(1, nx):
        k = lev_of(xm(d), y, core)
        lev_wait(k, A)
        for e in range(1, ny):
            lev_send(k, A, dev(z, x, ym(e), core))
        if nk > 1:
            lev_send(k, A, dev(z, x, y, other))
    for d in range(1, ny):
        k = lev_of(x, ym(d), core)
        lev_wait(k, B)
        for e in range(1, nx):
            lev_send(k, B, dev(z, xm(e), y, core))
        if nk > 1:
            lev_send(k, B, dev(z, x, y, other))
    z_round(1, 1)
    z_round(2, 0)
    z_round(1, 2)
    z_round(2, 1)
    z_round(1, 3)
    z_round(3, 0)
    for d in range(1, nx):
        k = lev_of(xm(d), y, core)
        lev_wait(k, B)
        if nk > 1:
            lev_send(k, B, dev(z, x, y, other))
    for d in range(1, ny):
        k = lev_of(x, ym(d), core)
        lev_wait(k, A)
        if nk > 1:
            lev_send(k, A, dev(z, x, y, other))
    z_round(2, 2)
    z_round(3, 1)
    z_round(2, 3)
    for d in range(1, nx):
        for e in range(1, ny):
            k = lev_of(xm(d), ym(e), core)
            for part in (A, B):
                lev_wait(k, part)
                if nk > 1:
                    lev_send(k, part, dev(z, x, y, other))
    z_round(3, 2)
    z_round(3, 3)
    if nk > 1:
        for d in range(nx):
            for e in range(ny):
                k = lev_of(xm(d), ym(e), other)
                for part in (A, B):
                    lev_wait(k, part)

    def prep_step(d, _):
        k = (me + d) % n_lev
        prep(k, RX[k], RL[k])
        return 0

    lax.fori_loop(1, n_lev, prep_step, 0)

    span = pn.group * blk
    scale = -1.0 / (2.0 * pn.width)

    def column(xv, lv, own):
        chi, clo = split(xv)
        nc = jnp.sum(xv * xv, axis=1, keepdims=True)
        lf = lv.astype(F32)
        l0 = lf[:, 0:1]
        proj = jnp.zeros((blk, pn.perms), F32)
        tot = jnp.zeros((1, blk), F32)
        for j in range(n_lev // pn.group):
            rows = pl.ds(j * span, span)
            hi, lo, lb = RHI[rows, :], RLO[rows, :], RLB[rows, :]
            dots = nt(chi, hi) + nt(chi, lo) + nt(clo, hi)
            dist = jnp.maximum(nc + NR[:, rows] - 2.0 * dots, 0.0)
            kern = jnp.exp(dist * scale)
            if own:
                ids = lax.broadcasted_iota(jnp.int32, (blk, span), 1) + j * span
                mine = lax.broadcasted_iota(jnp.int32, (blk, span), 0) + me * blk
                kern = jnp.where(ids == mine, 0.0, kern)
            kh, kl = split(kern)
            proj = proj + nn(kh, lb) + nn(kl, lb)
            t = jnp.sum(kern, axis=0, keepdims=True)
            for g in range(pn.group):
                tot = tot + t[:, g * blk:(g + 1) * blk]
            if not own:
                ROWP[:, rows] += jnp.sum(kern * l0, axis=0, keepdims=True)
        quad = jnp.sum(lf * proj, axis=0, keepdims=True)
        return quad, tot, to_row(proj[:, 0:1])

    ROWP[...] = jnp.zeros_like(ROWP)
    COLP[...] = jnp.zeros_like(COLP)
    quad, tot, own_proof = column(x_ref[...], l_ref[...], True)
    QUAD[...] = quad
    TOT[...] = tot
    for b in routes:
        d, h = routes[b]
        reach = [b + d * i for i in range(1, h + 1)]

        @pl.when((z >= min(reach)) & (z <= max(reach)))
        def _():
            q, t, pr = column(CX[b], CL[b], False)
            QUAD[...] += 2.0 * q
            TOT[...] += 2.0 * t
            COLP[b:b + 1, :] = pr

    qr = pn.perms // 128
    for k in range(n_lev):
        for i in range(qr):
            S1[k, i:i + 1, :] = QUAD[:, i * 128:(i + 1) * 128]
        S1[k, qr:qr + 1, :] = TOT[...]
        S1[k, qr + 1:qr + 2, :] = ROWP[:, k * blk:(k + 1) * blk]
        S1[k, qr + 2:, :] = jnp.zeros((S1.shape[1] - qr - 2, 128), F32)

    def s1_copy(d):
        k = (me + d) % n_lev
        return pltpu.make_async_remote_copy(
            src_ref=S1.at[k], dst_ref=R1.at[me], send_sem=s1_send.at[k], recv_sem=s1_recv.at[me],
            device_id=lev_dev(k), device_id_type=MESH)

    def s1_in(d):
        k = (me + d) % n_lev
        return pltpu.make_async_remote_copy(
            src_ref=S1.at[k], dst_ref=R1.at[k], send_sem=s1_send.at[k], recv_sem=s1_recv.at[k],
            device_id=lev_dev(k), device_id_type=MESH)

    for d in range(1, n_lev):
        s1_copy(d).start()
    acc = S1[me]
    for d in range(1, n_lev):
        s1_in(d).wait_recv()
        acc = acc + R1[(me + d) % n_lev]
    for b in range(nz):
        S2[b, :, :] = acc
        S2[b, qr + 1:qr + 2, :] = COLP[b:b + 1, :]

    def s2_copy(d):
        b = (z + d) % nz
        return pltpu.make_async_remote_copy(
            src_ref=S2.at[b], dst_ref=R2.at[z], send_sem=s2_send.at[b], recv_sem=s2_recv.at[z],
            device_id=dev(b, x, y, core), device_id_type=MESH)

    def s2_in(d):
        b = (z + d) % nz
        return pltpu.make_async_remote_copy(
            src_ref=S2.at[b], dst_ref=R2.at[b], send_sem=s2_send.at[b], recv_sem=s2_recv.at[b],
            device_id=dev(b, x, y, core), device_id_type=MESH)

    for d in range(1, nz):
        s2_copy(d).start()
    for d in range(1, nz):
        s2_in(d).wait_recv()
    tops = []
    extra = jnp.zeros((1, 128), F32)
    for b in range(nz):
        mine = z == b
        tops.append(jnp.where(mine, acc, R2[b]))
        extra = extra + jnp.where(mine, 0.0, R2[b, qr + 1:qr + 2, :])
    done = functools.reduce(lambda u, v: u + v, tops)
    proof = acc[qr + 1:qr + 2, :] + own_proof + extra
    total = jnp.sum(done[qr:qr + 1, :], axis=1, keepdims=True)
    hf = pn.rows / 2.0
    den = 2.0 * hf * (hf - 1.0)
    stat = total / den + ((2.0 * hf - 1.0) / den) * done[0:qr, :]
    stat_ref[...] = stat
    proof_ref[...] = proof / math.sqrt(pn.rows)
    sg = 1.0 / (1.0 + jnp.exp(-4.0 * (stat - stat[0:1, 0:1])))
    first = (lax.broadcasted_iota(jnp.int32, stat.shape, 0) + lax.broadcasted_iota(jnp.int32, stat.shape, 1)) == 0
    sg = jnp.where(first, 0.0, sg)
    p = jnp.sum(jnp.sum(sg, axis=0, keepdims=True), axis=1, keepdims=True) / (pn.perms - 1)
    p_ref[...] = p

    for c in pending:
        c.wait_send()
    for b, ch, at, own, sems in z_pending:
        @pl.when(z == at)
        def _():
            for c in z_copy(b, ch, dev(at + routes[b][0], x, y, core), own, sems):
                c.wait_send()
    for d in range(1, n_lev):
        s1_copy(d).wait_send()
    for d in range(1, nz):
        s2_copy(d).wait_send()
    assert counter[0] == n_send


def send_count(pn):
    nx, ny, nk, nz = pn.nx, pn.ny, pn.nk, pn.nz
    own = 2 * (nx - 1) + 2 * (ny - 1) + (2 if nk > 1 else 0)
    fwd = 2 * (nx - 1) * (ny - 1)
    core = 2 * (nx * ny - 1) if nk > 1 else 0
    line = sum(h for _, h in ROUTES[nz].values()) * CHUNKS
    return 2 * (own + fwd + core + line)


def solution(mesh):
    n_row, n_col = mesh.shape["row"], mesh.shape["col"]

    def shards(samples, labels):
        blk, width = samples.shape
        perms = labels.shape[1]
        pn = Plan(n_row, n_col, blk, width, perms)
        n_send = send_count(pn)
        n_lev, nz = pn.n_lev, pn.nz
        vm = pl.BlockSpec(memory_space=pltpu.VMEM)
        dma = pltpu.SemaphoreType.DMA
        stat, proof, p = pl.pallas_call(
            functools.partial(kernel, pn, n_send),
            out_shape=(
                jax.ShapeDtypeStruct((perms // 128, 128), F32),
                jax.ShapeDtypeStruct((1, blk), F32),
                jax.ShapeDtypeStruct((1, 1), F32),
            ),
            in_specs=[vm, vm],
            out_specs=(vm, vm, vm),
            scratch_shapes=[
                pltpu.VMEM((n_lev, blk, width), F32),
                pltpu.VMEM((n_lev, blk, perms), jnp.int32),
                pltpu.VMEM((nz, blk, width), F32),
                pltpu.VMEM((nz, blk, perms), jnp.int32),
                pltpu.VMEM((n_lev * blk, width), BF16),
                pltpu.VMEM((n_lev * blk, width), BF16),
                pltpu.VMEM((n_lev * blk, perms), BF16),
                pltpu.VMEM((1, n_lev * blk), F32),
                pltpu.VMEM((1, n_lev * blk), F32),
                pltpu.VMEM((1, perms), F32),
                pltpu.VMEM((1, blk), F32),
                pltpu.VMEM((nz, blk), F32),
                pltpu.VMEM((n_lev, 8, 128), F32),
                pltpu.VMEM((n_lev, 8, 128), F32),
                pltpu.VMEM((nz, 8, 128), F32),
                pltpu.VMEM((nz, 8, 128), F32),
                dma((n_send,)),
                dma((n_lev, 2 * PARTS)),
                dma((nz, 2 * CHUNKS)),
                dma((n_lev,)),
                dma((n_lev,)),
                dma((nz,)),
                dma((nz,)),
            ],
            compiler_params=pltpu.CompilerParams(
                collective_id=0, has_side_effects=True, vmem_limit_bytes=60 * 1024 * 1024
            ),
        )(samples, labels)
        return stat.reshape(perms), proof.reshape(blk), p.reshape(())

    placed = (P(("row", "col"), None), P(("row", "col"), None))
    return jax.shard_map(
        shards, mesh=mesh, in_specs=placed, out_specs=(P(), P(("row", "col")), P()), check_vma=False
    )
```

time: 181 us -> 46.4 us (0.26)
  waiting for transfers between devices: 90.9 us -> 0 us
  blocking collectives: 54.9 us -> 0 us
  Pallas kernels: 0 us -> 42 us
  between operations: 16.9 us -> 2.4 us
  matrix products: 9.2 us -> 0 us
  other arithmetic: 5.92 us -> 0 us
    all_gather x3 -> x0, waiting for transfers between devices: 89.5 us -> none  [the longest x1 49.9 us: shards(): lax.all_gather(samples, 'row', axis=0, tiled=True)]
    pallas_call x0 -> x1, Pallas kernels: none -> 42 us  [shards(): pl.pallas_call(functools.partial(kernel, pn, n_send), out_shape=(jax.Shap...]
    psum x1 -> x0, blocking collectives: 40.1 us -> none  [shards(): quad, total = lax.psum((quad, total), ('row', 'col'))]
    dot_general x2 -> x0, matrix products: 9.2 us -> none  [the longest x1 5.93 us: tile_terms(): lax.dot_general(xr, xc, (((1,), (1,)), ((), ())), precision=lax.Precision...]
    all_gather x1 -> x0, blocking collectives: 8.89 us -> none  [shards(): lax.all_gather(labs, 'col', axis=0, tiled=True)]
    unnamed x1 -> x0, blocking collectives: 5.98 us -> none
    reduce_sum x3 -> x0, other arithmetic: 4.65 us -> none  [the longest x1 1.96 us: tile_terms(): norm_cols = jnp.sum(xc * xc, 1)]
  transfers between devices with their start and end apart: 3 -> 0, of which waited for: 3 -> 0; matrix products, arithmetic and copies ran while one was open for 7% -> 0% of each run, Pallas kernels for 0% -> 0%
where the time goes in v1:
time: 46.4 us; the launch traced here: 46.2 us
  Pallas kernels  42 us (91%)
  between operations  2.4 us (5%)
  local copies, waits for them, and re-layouts  1.8 us (4%)
    pallas_call x1, Pallas kernels, shards(): pl.pallas_call(functools.partial(kernel, pn, n_send), out_shape=(jax.Shap...  42 us
    unnamed x6, local copies, waits for them, and re-layouts  1.8 us

profile of v1, /device:TPU:0, one launch (start us, length us, event | category | flops | bytes accessed | tf_op | source)
XLA Modules:
  0.0 46.2 jit_solution(13201530753958078865)
XLA Ops:
  0.6 42.0 %shard_map.49 = (f32[2,128]{1,0:T(2,128)}, f32[1,128]{1,0:T(1,128)}, f32[1,1]{1,0:T(1,128)}) custom-call(f32[128,512]{1,0:T(8,128)} %x_ref.1, s32[128,256]{1,0:T(8,128)} %l_ref.1), custom_call_target="tpu_custom_call" | custom-call | tf_op jit(solution)/shard_map/pallas_call | solution.py:381
  42.7 0.0 copy-start
  42.7 0.7 %copy-done = f32[2,128]{1,0:T(2,128)S(1)} copy-done((f32[2,128]{1,0:T(2,128)S(1)}, f32[2,128]{1,0:T(2,128)}, u32[]{:S(2)}) %copy-start) | copy-done | bytes 1048
  43.3 0.0 copy-start.1
  43.4 0.6 %copy.8 = f32[256]{0:T(256)} copy(f32[256]{0:T(256)S(1)} %bitcast.3) | data formatting | bytes 2048
  43.9 0.1 copy-done.1
  44.0 0.5 %copy.9 = f32[128]{0:T(128)} copy(f32[128]{0:T(128)S(1)} %bitcast.4) | data formatting | bytes 1024
Async XLA Ops:
  42.7 0.7 %copy-start = (f32[2,128]{1,0:T(2,128)S(1)}, f32[2,128]{1,0:T(2,128)}, u32[]{:S(2)}) copy-start(f32[2,128]{1,0:T(2,128)} %get-tuple-element.6) | copy-start | bytes 3076
  43.3 0.6 %copy-start.1 = (f32[1,128]{1,0:T(1,128)S(1)}, f32[1,128]{1,0:T(1,128)}, u32[]{:S(2)}) copy-start(f32[1,128]{1,0:T(1,128)} %get-tuple-element.7) | copy-start | bytes 1540

commit v2 on v1

--- a/solution.py
+++ b/solution.py
@@ -44,12 +44,12 @@
         self.n_col = n_col
         self.n_lev = self.nx * n_col
         self.blk, self.width, self.perms = blk, width, perms
-        self.group = math.gcd(self.n_lev, 4)
+        self.group = math.gcd(n_col, 4)
         self.rows = blk * n_row * n_col
 
 
 def kernel(pn, n_send, x_ref, l_ref, stat_ref, proof_ref, p_ref, RX, RL, CX, CL, RHI, RLO, RLB, NR,
-           ROWP, QUAD, TOT, COLP, S1, R1, S2, R2, send, lev_sem, z_sem, s1_send, s1_recv, s2_send, s2_recv):
+           ROWP, PROJ, QUAD, TOT, COLP, S1, R1, S2, R2, send, lev_sem, z_sem, s1_send, s1_recv, s2_send, s2_recv):
     nx, ny, nz, nk, n_col, n_lev, blk = pn.nx, pn.ny, pn.nz, pn.nk, pn.n_col, pn.n_lev, pn.blk
     row, col = lax.axis_index("row"), lax.axis_index("col")
     z, x = row // nx, row % nx
@@ -124,15 +124,19 @@
                 c.start()
         z_pending.append((b, ch, at, own, sems))
 
-    def z_event(b, ch, hop):
-        at = b + routes[b][0] * hop
-
-        @pl.when(z == at)
-        def _():
-            for c in z_copy(b, ch, (row, col), False, [send.at[0]] * 2):
-                c.wait_recv()
-        if hop < routes[b][1]:
-            z_send(b, ch, at, False)
+    def z_arrive(b, ch, at):
+        for c in z_copy(b, ch, (row, col), False, [send.at[0]] * 2):
+            c.wait_recv()
+
+    def z_round(hop, ch):
+        for b in routes:
+            if hop < routes[b][1]:
+                at = b + routes[b][0] * hop
+
+                @pl.when(z == at)
+                def _():
+                    z_arrive(b, ch, at)
+                z_send(b, ch, at, False)
 
     def xm(d):
         return (x + d) % nx
@@ -165,91 +169,32 @@
         RLB[rows, :] = lv.astype(F32).astype(BF16)
         NR[:, rows] = to_row(jnp.sum(xv * xv, axis=1, keepdims=True))
 
-    prep(me, x_ref[...], l_ref[...])
-
-    def hops(b):
-        return routes[b][1]
-
-    def z_round(hop, ch):
-        for b in routes:
-            if hop <= hops(b):
-                z_event(b, ch, hop)
-
-    z_round(1, 0)
-    for d in range(1, nx):
-        k = lev_of(xm(d), y, core)
-        lev_wait(k, A)
-        for e in range(1, ny):
-            lev_send(k, A, dev(z, x, ym(e), core))
-        if nk > 1:
-            lev_send(k, A, dev(z, x, y, other))
-    for d in range(1, ny):
-        k = lev_of(x, ym(d), core)
-        lev_wait(k, B)
-        for e in range(1, nx):
-            lev_send(k, B, dev(z, xm(e), y, core))
-        if nk > 1:
-            lev_send(k, B, dev(z, x, y, other))
-    z_round(1, 1)
-    z_round(2, 0)
-    z_round(1, 2)
-    z_round(2, 1)
-    z_round(1, 3)
-    z_round(3, 0)
-    for d in range(1, nx):
-        k = lev_of(xm(d), y, core)
-        lev_wait(k, B)
-        if nk > 1:
-            lev_send(k, B, dev(z, x, y, other))
-    for d in range(1, ny):
-        k = lev_of(x, ym(d), core)
-        lev_wait(k, A)
-        if nk > 1:
-            lev_send(k, A, dev(z, x, y, other))
-    z_round(2, 2)
-    z_round(3, 1)
-    z_round(2, 3)
-    for d in range(1, nx):
-        for e in range(1, ny):
-            k = lev_of(xm(d), ym(e), core)
-            for part in (A, B):
-                lev_wait(k, part)
-                if nk > 1:
-                    lev_send(k, part, dev(z, x, y, other))
-    z_round(3, 2)
-    z_round(3, 3)
-    if nk > 1:
-        for d in range(nx):
-            for e in range(ny):
-                k = lev_of(xm(d), ym(e), other)
-                for part in (A, B):
-                    lev_wait(k, part)
-
-    def prep_step(d, _):
-        k = (me + d) % n_lev
-        prep(k, RX[k], RL[k])
-        return 0
-
-    lax.fori_loop(1, n_lev, prep_step, 0)
+    def prep_chunk(xx, skip):
+        def step(i, _):
+            k = xx * n_col + (col + i) % n_col
+            prep(k, RX[k], RL[k])
+            return 0
+
+        lax.fori_loop(skip, n_col, step, 0)
 
     span = pn.group * blk
     scale = -1.0 / (2.0 * pn.width)
 
-    def column(xv, lv, own):
+    def tile(slot, xx, xv, lv, own):
         chi, clo = split(xv)
         nc = jnp.sum(xv * xv, axis=1, keepdims=True)
-        lf = lv.astype(F32)
-        l0 = lf[:, 0:1]
-        proj = jnp.zeros((blk, pn.perms), F32)
-        tot = jnp.zeros((1, blk), F32)
-        for j in range(n_lev // pn.group):
-            rows = pl.ds(j * span, span)
+        l0 = lv[:, 0:1].astype(F32)
+        proj = PROJ[slot]
+        tot = TOT[slot:slot + 1, :]
+        for j in range(n_col // pn.group):
+            base = pl.multiple_of(xx * n_col * blk + j * span, span)
+            rows = pl.ds(base, span)
             hi, lo, lb = RHI[rows, :], RLO[rows, :], RLB[rows, :]
             dots = nt(chi, hi) + nt(chi, lo) + nt(clo, hi)
             dist = jnp.maximum(nc + NR[:, rows] - 2.0 * dots, 0.0)
             kern = jnp.exp(dist * scale)
             if own:
-                ids = lax.broadcasted_iota(jnp.int32, (blk, span), 1) + j * span
+                ids = lax.broadcasted_iota(jnp.int32, (blk, span), 1) + base
                 mine = lax.broadcasted_iota(jnp.int32, (blk, span), 0) + me * blk
                 kern = jnp.where(ids == mine, 0.0, kern)
             kh, kl = split(kern)
@@ -259,30 +204,110 @@
                 tot = tot + t[:, g * blk:(g + 1) * blk]
             if not own:
                 ROWP[:, rows] += jnp.sum(kern * l0, axis=0, keepdims=True)
-        quad = jnp.sum(lf * proj, axis=0, keepdims=True)
-        return quad, tot, to_row(proj[:, 0:1])
-
+        PROJ[slot] = proj
+        TOT[slot:slot + 1, :] = tot
+
+    def line_tiles(hop, chunks, arrive):
+        for b in routes:
+            if hop <= routes[b][1]:
+                at = b + routes[b][0] * hop
+
+                @pl.when(z == at)
+                def _():
+                    if arrive and hop == routes[b][1]:
+                        for ch in range(CHUNKS):
+                            z_arrive(b, ch, at)
+                    for xx in chunks:
+                        tile(b, xx, CX[b], CL[b], False)
+
+    def own_tile(xx):
+        tile(nz, xx, x_ref[...], l_ref[...], True)
+
+    prep(me, x_ref[...], l_ref[...])
     ROWP[...] = jnp.zeros_like(ROWP)
-    COLP[...] = jnp.zeros_like(COLP)
-    quad, tot, own_proof = column(x_ref[...], l_ref[...], True)
-    QUAD[...] = quad
-    TOT[...] = tot
-    for b in routes:
-        d, h = routes[b]
-        reach = [b + d * i for i in range(1, h + 1)]
-
-        @pl.when((z >= min(reach)) & (z <= max(reach)))
+    PROJ[...] = jnp.zeros_like(PROJ)
+    TOT[...] = jnp.zeros_like(TOT)
+
+    def partner(k, part):
+        if nk > 1:
+            lev_send(k, part, dev(z, x, y, other))
+
+    z_round(1, 0)
+    for d in range(1, nx):
+        k = lev_of(xm(d), y, core)
+        lev_wait(k, A)
+        for e in range(1, ny):
+            lev_send(k, A, dev(z, x, ym(e), core))
+        partner(k, A)
+    for d in range(1, ny):
+        k = lev_of(x, ym(d), core)
+        lev_wait(k, B)
+        for e in range(1, nx):
+            lev_send(k, B, dev(z, xm(e), y, core))
+        partner(k, B)
+    z_round(1, 1)
+    z_round(2, 0)
+    z_round(1, 2)
+    z_round(2, 1)
+    z_round(1, 3)
+    for d in range(1, ny):
+        k = lev_of(x, ym(d), core)
+        lev_wait(k, A)
+        partner(k, A)
+    for d in range(1, nx):
+        k = lev_of(xm(d), y, core)
+        lev_wait(k, B)
+        partner(k, B)
+    z_round(2, 2)
+
+    def other_core(xx, ys):
+        if nk > 1:
+            for e in ys:
+                for part in (A, B):
+                    lev_wait(lev_of(xx, ym(e), other), part)
+
+    other_core(x, range(ny))
+    prep_chunk(x, 1)
+    own_tile(x)
+    z_round(2, 3)
+    line_tiles(1, [x], True)
+    for d in range(1, nx):
+        for e in range(1, ny):
+            k = lev_of(xm(d), ym(e), core)
+            for part in (A, B):
+                lev_wait(k, part)
+                partner(k, part)
+    far = [xm(d) for d in range(1, nx)]
+    for xx in far:
+        other_core(xx, range(ny))
+        prep_chunk(xx, 0)
+        own_tile(xx)
+    line_tiles(1, far, False)
+    for hop in range(2, nz):
+        line_tiles(hop, [x] + far, True)
+
+    quad = jnp.zeros((1, pn.perms), F32)
+    tot = jnp.zeros((1, blk), F32)
+    for b in list(routes) + [nz]:
+        w = 1.0 if b == nz else 2.0
+        lv = l_ref[...] if b == nz else CL[b]
+        QUAD[b:b + 1, :] = jnp.zeros((1, pn.perms), F32)
+        COLP[b:b + 1, :] = jnp.zeros((1, blk), F32)
+        reach = [nz - 1] if b == nz else [b + routes[b][0] * h for h in range(1, routes[b][1] + 1)]
+
+        @pl.when((z >= (0 if b == nz else min(reach))) & (z <= max(reach)))
         def _():
-            q, t, pr = column(CX[b], CL[b], False)
-            QUAD[...] += 2.0 * q
-            TOT[...] += 2.0 * t
-            COLP[b:b + 1, :] = pr
+            QUAD[b:b + 1, :] = w * jnp.sum(lv.astype(F32) * PROJ[b], axis=0, keepdims=True)
+            COLP[b:b + 1, :] = to_row(PROJ[b][:, 0:1])
+        quad = quad + QUAD[b:b + 1, :]
+        tot = tot + w * TOT[b:b + 1, :]
+    own_proof = COLP[nz:nz + 1, :]
 
     qr = pn.perms // 128
     for k in range(n_lev):
         for i in range(qr):
-            S1[k, i:i + 1, :] = QUAD[:, i * 128:(i + 1) * 128]
-        S1[k, qr:qr + 1, :] = TOT[...]
+            S1[k, i:i + 1, :] = quad[:, i * 128:(i + 1) * 128]
+        S1[k, qr:qr + 1, :] = tot
         S1[k, qr + 1:qr + 2, :] = ROWP[:, k * blk:(k + 1) * blk]
         S1[k, qr + 2:, :] = jnp.zeros((S1.shape[1] - qr - 2, 128), F32)
 
@@ -306,7 +331,7 @@
         acc = acc + R1[(me + d) % n_lev]
     for b in range(nz):
         S2[b, :, :] = acc
-        S2[b, qr + 1:qr + 2, :] = COLP[b:b + 1, :]
+        S2[b, qr + 1:qr + 2, :] = COLP[b:b + 1, :] if b in routes else jnp.zeros((1, 128), F32)
 
     def s2_copy(d):
         b = (z + d) % nz
@@ -397,9 +422,10 @@
                 pltpu.VMEM((n_lev * blk, perms), BF16),
                 pltpu.VMEM((1, n_lev * blk), F32),
                 pltpu.VMEM((1, n_lev * blk), F32),
-                pltpu.VMEM((1, perms), F32),
-                pltpu.VMEM((1, blk), F32),
-                pltpu.VMEM((nz, blk), F32),
+                pltpu.VMEM((nz + 1, blk, perms), F32),
+                pltpu.VMEM((nz + 1, perms), F32),
+                pltpu.VMEM((nz + 1, blk), F32),
+                pltpu.VMEM((nz + 1, blk), F32),
                 pltpu.VMEM((n_lev, 8, 128), F32),
                 pltpu.VMEM((n_lev, 8, 128), F32),
                 pltpu.VMEM((nz, 8, 128), F32),

time: 46.4 us -> 40.9 us (0.88)
  Pallas kernels: 42 us -> 36.5 us
    pallas_call x1, Pallas kernels: 42 us -> 36.5 us  [shards(): pl.pallas_call(functools.partial(kernel, pn, n_send), out_shape=(jax.Shap...]
where the time goes in v2:
time: 40.9 us; the launch traced here: 40.7 us
  Pallas kernels  36.5 us (89%)
  between operations  2.4 us (6%)
  local copies, waits for them, and re-layouts  1.8 us (4%)
    pallas_call x1, Pallas kernels, shards(): pl.pallas_call(functools.partial(kernel, pn, n_send), out_shape=(jax.Shap...  36.5 us
    unnamed x6, local copies, waits for them, and re-layouts  1.8 us

profile of v2, /device:TPU:0, one launch (start us, length us, event | category | flops | bytes accessed | tf_op | source)
XLA Modules:
  0.0 40.7 jit_solution(5853553002657346200)
XLA Ops:
  0.6 36.5 %shard_map.49 = (f32[2,128]{1,0:T(2,128)}, f32[1,128]{1,0:T(1,128)}, f32[1,1]{1,0:T(1,128)}) custom-call(f32[128,512]{1,0:T(8,128)} %x_ref.1, s32[128,256]{1,0:T(8,128)} %l_ref.1), custom_call_target="tpu_custom_call" | custom-call | tf_op jit(solution)/shard_map/pallas_call | solution.py:406
  37.1 0.0 copy-start
  37.1 0.7 %copy-done = f32[2,128]{1,0:T(2,128)S(1)} copy-done((f32[2,128]{1,0:T(2,128)S(1)}, f32[2,128]{1,0:T(2,128)}, u32[]{:S(2)}) %copy-start) | copy-done | bytes 1048
  37.8 0.0 copy-start.1
  37.8 0.6 %copy.8 = f32[256]{0:T(256)} copy(f32[256]{0:T(256)S(1)} %bitcast.3) | data formatting | bytes 2048
  38.3 0.1 copy-done.1
  38.4 0.5 %copy.9 = f32[128]{0:T(128)} copy(f32[128]{0:T(128)S(1)} %bitcast.4) | data formatting | bytes 1024
Async XLA Ops:
  37.1 0.7 %copy-start = (f32[2,128]{1,0:T(2,128)S(1)}, f32[2,128]{1,0:T(2,128)}, u32[]{:S(2)}) copy-start(f32[2,128]{1,0:T(2,128)} %get-tuple-element.6) | copy-start | bytes 3076
  37.8 0.6 %copy-start.1 = (f32[1,128]{1,0:T(1,128)S(1)}, f32[1,128]{1,0:T(1,128)}, u32[]{:S(2)}) copy-start(f32[1,128]{1,0:T(1,128)} %get-tuple-element.7) | copy-start | bytes 1540

commit v3 on v2

--- a/solution.py
+++ b/solution.py
@@ -44,12 +44,13 @@
         self.n_col = n_col
         self.n_lev = self.nx * n_col
         self.blk, self.width, self.perms = blk, width, perms
+        self.direct = n_row * n_col <= 32
         self.group = math.gcd(n_col, 4)
         self.rows = blk * n_row * n_col
 
 
 def kernel(pn, n_send, x_ref, l_ref, stat_ref, proof_ref, p_ref, RX, RL, CX, CL, RHI, RLO, RLB, NR,
-           ROWP, PROJ, QUAD, TOT, COLP, S1, R1, S2, R2, send, lev_sem, z_sem, s1_send, s1_recv, s2_send, s2_recv):
+           ROWP, PROJ, QUAD, TOT, COLP, S1, R1, S2, R2, send, lev_sem, z_sem, s1_send, s1_recv, s2_send, s2_recv, here):
     nx, ny, nz, nk, n_col, n_lev, blk = pn.nx, pn.ny, pn.nz, pn.nk, pn.n_col, pn.n_lev, pn.blk
     row, col = lax.axis_index("row"), lax.axis_index("col")
     z, x = row // nx, row % nx
@@ -73,6 +74,12 @@
     for d in range(1, nz):
         pl.semaphore_signal(barrier, inc=1, device_id=dev((z + d) % nz, x, y, core), device_id_type=MESH)
     pl.semaphore_wait(barrier, n_lev - 1 + nz - 1)
+
+    n_dev = nz * n_lev
+    direct = pn.direct
+    if direct:
+        for d in range(1, nz):
+            pl.semaphore_signal(here, inc=1, device_id=dev((z + d) % nz, x, y, core), device_id_type=MESH)
 
     counter = [0]
 
@@ -304,59 +311,95 @@
     own_proof = COLP[nz:nz + 1, :]
 
     qr = pn.perms // 128
-    for k in range(n_lev):
-        for i in range(qr):
-            S1[k, i:i + 1, :] = quad[:, i * 128:(i + 1) * 128]
-        S1[k, qr:qr + 1, :] = tot
-        S1[k, qr + 1:qr + 2, :] = ROWP[:, k * blk:(k + 1) * blk]
-        S1[k, qr + 2:, :] = jnp.zeros((S1.shape[1] - qr - 2, 128), F32)
-
-    def s1_copy(d):
-        k = (me + d) % n_lev
-        return pltpu.make_async_remote_copy(
-            src_ref=S1.at[k], dst_ref=R1.at[me], send_sem=s1_send.at[k], recv_sem=s1_recv.at[me],
-            device_id=lev_dev(k), device_id_type=MESH)
-
-    def s1_in(d):
-        k = (me + d) % n_lev
-        return pltpu.make_async_remote_copy(
-            src_ref=S1.at[k], dst_ref=R1.at[k], send_sem=s1_send.at[k], recv_sem=s1_recv.at[k],
-            device_id=lev_dev(k), device_id_type=MESH)
-
-    for d in range(1, n_lev):
-        s1_copy(d).start()
-    acc = S1[me]
-    for d in range(1, n_lev):
-        s1_in(d).wait_recv()
-        acc = acc + R1[(me + d) % n_lev]
-    for b in range(nz):
-        S2[b, :, :] = acc
-        S2[b, qr + 1:qr + 2, :] = COLP[b:b + 1, :] if b in routes else jnp.zeros((1, 128), F32)
-
-    def s2_copy(d):
-        b = (z + d) % nz
-        return pltpu.make_async_remote_copy(
-            src_ref=S2.at[b], dst_ref=R2.at[z], send_sem=s2_send.at[b], recv_sem=s2_recv.at[z],
-            device_id=dev(b, x, y, core), device_id_type=MESH)
-
-    def s2_in(d):
-        b = (z + d) % nz
-        return pltpu.make_async_remote_copy(
-            src_ref=S2.at[b], dst_ref=R2.at[b], send_sem=s2_send.at[b], recv_sem=s2_recv.at[b],
-            device_id=dev(b, x, y, core), device_id_type=MESH)
-
-    for d in range(1, nz):
-        s2_copy(d).start()
-    for d in range(1, nz):
-        s2_in(d).wait_recv()
-    tops = []
-    extra = jnp.zeros((1, 128), F32)
-    for b in range(nz):
-        mine = z == b
-        tops.append(jnp.where(mine, acc, R2[b]))
-        extra = extra + jnp.where(mine, 0.0, R2[b, qr + 1:qr + 2, :])
-    done = functools.reduce(lambda u, v: u + v, tops)
-    proof = acc[qr + 1:qr + 2, :] + own_proof + extra
+    if direct:
+        def head(ref, i):
+            for j in range(qr):
+                ref[i, j:j + 1, :] = quad[:, j * 128:(j + 1) * 128]
+            ref[i, qr:qr + 1, :] = tot
+
+        index = z * n_lev + me
+        none = jnp.zeros((1, 128), F32)
+        for k in range(n_lev):
+            head(S1, k)
+            S1[k, qr + 1:qr + 2, :] = ROWP[:, k * blk:(k + 1) * blk]
+        for b in range(nz):
+            head(S2, b)
+            S2[b, qr + 1:qr + 2, :] = COLP[b:b + 1, :] if b in routes else none
+        head(S2, nz)
+        S2[nz, qr + 1:qr + 2, :] = none
+        if nz > 1:
+            pl.semaphore_wait(here, nz - 1)
+
+        def x_copy(dz, d, slot):
+            b, k = (z + dz) % nz, (me + d) % n_lev
+            src = S1.at[k] if dz == 0 else (S2.at[b] if d == 0 else S2.at[nz])
+            return pltpu.make_async_remote_copy(
+                src_ref=src, dst_ref=R1.at[slot], send_sem=s1_send.at[dz * n_lev + d], recv_sem=s1_recv.at[slot],
+                device_id=(b * nx + k // n_col, k % n_col), device_id_type=MESH)
+
+        pairs = [(dz, d) for dz in reversed(range(nz)) for d in range(n_lev) if dz + d > 0]
+        for dz, d in pairs:
+            x_copy(dz, d, index).start()
+        R1[index] = S1[me]
+        for dz, d in pairs:
+            x_copy(dz, d, ((z + dz) % nz) * n_lev + (me + d) % n_lev).wait_recv()
+        done = R1[0]
+        for i in range(1, n_dev):
+            done = done + R1[i]
+        proof = done[qr + 1:qr + 2, :] + own_proof
+    else:
+        for k in range(n_lev):
+            for i in range(qr):
+                S1[k, i:i + 1, :] = quad[:, i * 128:(i + 1) * 128]
+            S1[k, qr:qr + 1, :] = tot
+            S1[k, qr + 1:qr + 2, :] = ROWP[:, k * blk:(k + 1) * blk]
+
+        def s1_copy(d):
+            k = (me + d) % n_lev
+            return pltpu.make_async_remote_copy(
+                src_ref=S1.at[k], dst_ref=R1.at[me], send_sem=s1_send.at[k], recv_sem=s1_recv.at[me],
+                device_id=lev_dev(k), device_id_type=MESH)
+
+        def s1_in(d):
+            k = (me + d) % n_lev
+            return pltpu.make_async_remote_copy(
+                src_ref=S1.at[k], dst_ref=R1.at[k], send_sem=s1_send.at[k], recv_sem=s1_recv.at[k],
+                device_id=lev_dev(k), device_id_type=MESH)
+
+        for d in range(1, n_lev):
+            s1_copy(d).start()
+        acc = S1[me]
+        for d in range(1, n_lev):
+            s1_in(d).wait_recv()
+            acc = acc + R1[(me + d) % n_lev]
+        for b in range(nz):
+            S2[b, :, :] = acc
+            S2[b, qr + 1:qr + 2, :] = COLP[b:b + 1, :] if b in routes else jnp.zeros((1, 128), F32)
+
+        def s2_copy(d):
+            b = (z + d) % nz
+            return pltpu.make_async_remote_copy(
+                src_ref=S2.at[b], dst_ref=R2.at[z], send_sem=s2_send.at[b], recv_sem=s2_recv.at[z],
+                device_id=dev(b, x, y, core), device_id_type=MESH)
+
+        def s2_in(d):
+            b = (z + d) % nz
+            return pltpu.make_async_remote_copy(
+                src_ref=S2.at[b], dst_ref=R2.at[b], send_sem=s2_send.at[b], recv_sem=s2_recv.at[b],
+                device_id=dev(b, x, y, core), device_id_type=MESH)
+
+        for d in range(1, nz):
+            s2_copy(d).start()
+        for d in range(1, nz):
+            s2_in(d).wait_recv()
+        tops = []
+        extra = jnp.zeros((1, 128), F32)
+        for b in range(nz):
+            mine = z == b
+            tops.append(jnp.where(mine, acc, R2[b]))
+            extra = extra + jnp.where(mine, 0.0, R2[b, qr + 1:qr + 2, :])
+        done = functools.reduce(lambda u, v: u + v, tops)
+        proof = acc[qr + 1:qr + 2, :] + own_proof + extra
     total = jnp.sum(done[qr:qr + 1, :], axis=1, keepdims=True)
     hf = pn.rows / 2.0
     den = 2.0 * hf * (hf - 1.0)
@@ -376,10 +419,14 @@
         def _():
             for c in z_copy(b, ch, dev(at + routes[b][0], x, y, core), own, sems):
                 c.wait_send()
-    for d in range(1, n_lev):
-        s1_copy(d).wait_send()
-    for d in range(1, nz):
-        s2_copy(d).wait_send()
+    if direct:
+        for dz, d in pairs:
+            x_copy(dz, d, index).wait_send()
+    else:
+        for d in range(1, n_lev):
+            s1_copy(d).wait_send()
+        for d in range(1, nz):
+            s2_copy(d).wait_send()
     assert counter[0] == n_send
 
 
@@ -401,6 +448,8 @@
         pn = Plan(n_row, n_col, blk, width, perms)
         n_send = send_count(pn)
         n_lev, nz = pn.n_lev, pn.nz
+        msg = perms // 128 + 2
+        slots = n_row * n_col if pn.direct else n_lev
         vm = pl.BlockSpec(memory_space=pltpu.VMEM)
         dma = pltpu.SemaphoreType.DMA
         stat, proof, p = pl.pallas_call(
@@ -426,17 +475,18 @@
                 pltpu.VMEM((nz + 1, perms), F32),
                 pltpu.VMEM((nz + 1, blk), F32),
                 pltpu.VMEM((nz + 1, blk), F32),
-                pltpu.VMEM((n_lev, 8, 128), F32),
-                pltpu.VMEM((n_lev, 8, 128), F32),
-                pltpu.VMEM((nz, 8, 128), F32),
-                pltpu.VMEM((nz, 8, 128), F32),
+                pltpu.VMEM((n_lev, msg, 128), F32),
+                pltpu.VMEM((slots, msg, 128), F32),
+                pltpu.VMEM((nz + 1, msg, 128), F32),
+                pltpu.VMEM((nz, msg, 128), F32),
                 dma((n_send,)),
                 dma((n_lev, 2 * PARTS)),
                 dma((nz, 2 * CHUNKS)),
-                dma((n_lev,)),
-                dma((n_lev,)),
+                dma((slots,)),
+                dma((slots,)),
                 dma((nz,)),
                 dma((nz,)),
+                pltpu.SemaphoreType.REGULAR,
             ],
             compiler_params=pltpu.CompilerParams(
                 collective_id=0, has_side_effects=True, vmem_limit_bytes=60 * 1024 * 1024

time: 40.9 us -> 39.6 us (0.968)
  Pallas kernels: 36.5 us -> 35.2 us
    pallas_call x1, Pallas kernels: 36.5 us -> 35.2 us  [shards(): pl.pallas_call(functools.partial(kernel, pn, n_send), out_shape=(jax.Shap...]
where the time goes in v3:
time: 39.6 us; the launch traced here: 39.4 us
  Pallas kernels  35.2 us (89%)
  between operations  2.4 us (6%)
  local copies, waits for them, and re-layouts  1.8 us (5%)
    pallas_call x1, Pallas kernels, shards(): pl.pallas_call(functools.partial(kernel, pn, n_send), out_shape=(jax.Shap...  35.2 us
    unnamed x6, local copies, waits for them, and re-layouts  1.8 us

profile of v3, /device:TPU:0, one launch (start us, length us, event | category | flops | bytes accessed | tf_op | source)
XLA Modules:
  0.0 39.4 jit_solution(11402088100749437747)
XLA Ops:
  0.6 35.2 %shard_map.49 = (f32[2,128]{1,0:T(2,128)}, f32[1,128]{1,0:T(1,128)}, f32[1,1]{1,0:T(1,128)}) custom-call(f32[128,512]{1,0:T(8,128)} %x_ref.1, s32[128,256]{1,0:T(8,128)} %l_ref.1), custom_call_target="tpu_custom_call" | custom-call | tf_op jit(solution)/shard_map/pallas_call | solution.py:455
  35.9 0.0 copy-start
  35.9 0.7 %copy-done = f32[2,128]{1,0:T(2,128)S(1)} copy-done((f32[2,128]{1,0:T(2,128)S(1)}, f32[2,128]{1,0:T(2,128)}, u32[]{:S(2)}) %copy-start) | copy-done | bytes 1048
  36.5 0.0 copy-start.1
  36.5 0.6 %copy.8 = f32[256]{0:T(256)} copy(f32[256]{0:T(256)S(1)} %bitcast.3) | data formatting | bytes 2048
  37.1 0.1 copy-done.1
  37.2 0.5 %copy.9 = f32[128]{0:T(128)} copy(f32[128]{0:T(128)S(1)} %bitcast.4) | data formatting | bytes 1024
Async XLA Ops:
  35.9 0.7 %copy-start = (f32[2,128]{1,0:T(2,128)S(1)}, f32[2,128]{1,0:T(2,128)}, u32[]{:S(2)}) copy-start(f32[2,128]{1,0:T(2,128)} %get-tuple-element.6) | copy-start | bytes 3076
  36.5 0.6 %copy-start.1 = (f32[1,128]{1,0:T(1,128)S(1)}, f32[1,128]{1,0:T(1,128)}, u32[]{:S(2)}) copy-start(f32[1,128]{1,0:T(1,128)} %get-tuple-element.7) | copy-start | bytes 1540

commit v4 on v3

--- a/solution.py
+++ b/solution.py
@@ -49,8 +49,8 @@
         self.rows = blk * n_row * n_col
 
 
-def kernel(pn, n_send, x_ref, l_ref, stat_ref, proof_ref, p_ref, RX, RL, CX, CL, RHI, RLO, RLB, NR,
-           ROWP, PROJ, QUAD, TOT, COLP, S1, R1, S2, R2, send, lev_sem, z_sem, s1_send, s1_recv, s2_send, s2_recv, here):
+def kernel(pn, n_send, x_hbm, l_hbm, stat_ref, proof_ref, p_ref, x_ref, l_ref, RX, RL, CX, CL, RHI, RLO, RLB, NR,
+           ROWP, PROJ, QUAD, TOT, COLP, S1, R1, S2, R2, in_sem, send, lev_sem, z_sem, s1_send, s1_recv, s2_send, s2_recv, here):
     nx, ny, nz, nk, n_col, n_lev, blk = pn.nx, pn.ny, pn.nz, pn.nk, pn.n_col, pn.n_lev, pn.blk
     row, col = lax.axis_index("row"), lax.axis_index("col")
     z, x = row // nx, row % nx
@@ -68,12 +68,17 @@
     def lev_dev(k):
         return (z * nx + k // n_col, k % n_col)
 
+    loads = [pltpu.make_async_copy(x_hbm, x_ref, in_sem.at[0]), pltpu.make_async_copy(l_hbm, l_ref, in_sem.at[1])]
+    for c in loads:
+        c.start()
     barrier = pltpu.get_barrier_semaphore()
     for d in range(1, n_lev):
         pl.semaphore_signal(barrier, inc=1, device_id=lev_dev((me + d) % n_lev), device_id_type=MESH)
     for d in range(1, nz):
         pl.semaphore_signal(barrier, inc=1, device_id=dev((z + d) % nz, x, y, core), device_id_type=MESH)
     pl.semaphore_wait(barrier, n_lev - 1 + nz - 1)
+    for c in loads:
+        c.wait()
 
     n_dev = nz * n_lev
     direct = pn.direct
@@ -451,6 +456,7 @@
         msg = perms // 128 + 2
         slots = n_row * n_col if pn.direct else n_lev
         vm = pl.BlockSpec(memory_space=pltpu.VMEM)
+        hbm = pl.BlockSpec(memory_space=pl.ANY)
         dma = pltpu.SemaphoreType.DMA
         stat, proof, p = pl.pallas_call(
             functools.partial(kernel, pn, n_send),
@@ -459,9 +465,11 @@
                 jax.ShapeDtypeStruct((1, blk), F32),
                 jax.ShapeDtypeStruct((1, 1), F32),
             ),
-            in_specs=[vm, vm],
+            in_specs=[hbm, hbm],
             out_specs=(vm, vm, vm),
             scratch_shapes=[
+                pltpu.VMEM((blk, width), F32),
+                pltpu.VMEM((blk, perms), jnp.int32),
                 pltpu.VMEM((n_lev, blk, width), F32),
                 pltpu.VMEM((n_lev, blk, perms), jnp.int32),
                 pltpu.VMEM((nz, blk, width), F32),
@@ -479,6 +487,7 @@
                 pltpu.VMEM((slots, msg, 128), F32),
                 pltpu.VMEM((nz + 1, msg, 128), F32),
                 pltpu.VMEM((nz, msg, 128), F32),
+                dma((2,)),
                 dma((n_send,)),
                 dma((n_lev, 2 * PARTS)),
                 dma((nz, 2 * CHUNKS)),

time: 39.6 us -> 38.8 us (0.980)
  Pallas kernels: 35.2 us -> 34.4 us
    pallas_call x1, Pallas kernels: 35.2 us -> 34.4 us  [shards(): pl.pallas_call(functools.partial(kernel, pn, n_send), out_shape=(jax.Shap...]
where the time goes in v4:
time: 38.8 us; the launch traced here: 38.6 us
  Pallas kernels  34.4 us (89%)
  between operations  2.4 us (6%)
  local copies, waits for them, and re-layouts  1.8 us (5%)
    pallas_call x1, Pallas kernels, shards(): pl.pallas_call(functools.partial(kernel, pn, n_send), out_shape=(jax.Shap...  34.4 us
    unnamed x6, local copies, waits for them, and re-layouts  1.8 us

profile of v4, /device:TPU:0, one launch (start us, length us, event | category | flops | bytes accessed | tf_op | source)
XLA Modules:
  0.0 38.6 jit_solution(17229138267163226869)
XLA Ops:
  0.6 34.4 %shard_map.49 = (f32[2,128]{1,0:T(2,128)}, f32[1,128]{1,0:T(1,128)}, f32[1,1]{1,0:T(1,128)}) custom-call(f32[128,512]{1,0:T(8,128)} %x_hbm.1, s32[128,256]{1,0:T(8,128)} %l_hbm.1), custom_call_target="tpu_custom_call" | custom-call | tf_op jit(solution)/shard_map/pallas_call | solution.py:461
  35.1 0.0 copy-start
  35.1 0.7 %copy-done = f32[2,128]{1,0:T(2,128)S(1)} copy-done((f32[2,128]{1,0:T(2,128)S(1)}, f32[2,128]{1,0:T(2,128)}, u32[]{:S(2)}) %copy-start) | copy-done | bytes 1048
  35.7 0.0 copy-start.1
  35.7 0.6 %copy.8 = f32[256]{0:T(256)} copy(f32[256]{0:T(256)S(1)} %bitcast.3) | data formatting | bytes 2048
  36.3 0.1 copy-done.1
  36.4 0.5 %copy.9 = f32[128]{0:T(128)} copy(f32[128]{0:T(128)S(1)} %bitcast.4) | data formatting | bytes 1024
Async XLA Ops:
  35.1 0.7 %copy-start = (f32[2,128]{1,0:T(2,128)S(1)}, f32[2,128]{1,0:T(2,128)}, u32[]{:S(2)}) copy-start(f32[2,128]{1,0:T(2,128)} %get-tuple-element.6) | copy-start | bytes 3076
  35.7 0.6 %copy-start.1 = (f32[1,128]{1,0:T(1,128)S(1)}, f32[1,128]{1,0:T(1,128)}, u32[]{:S(2)}) copy-start(f32[1,128]{1,0:T(1,128)} %get-tuple-element.7) | copy-start | bytes 1540
